TPU v7x, 256 devices: a whole 4x4x8 slice. The times are simulated.
256 devices in a mesh: dp: 64 (over x, z_lo, y), expert: 4 (over z_hi, core).
Axes of the slice: x: 4, y: 4, z: 8 (z_hi: 2, z_lo: 4; z = z_hi * 4 + z_lo), core: 2. Of those that a mesh axis runs over, the one named last changes fastest.
Arguments:
- master: float32 [4, 7168, 2048], P('expert', 'dp'), may hold values from -6 to 6
- first_moment: float32 [4, 7168, 2048], P('expert', 'dp'), may hold values from -0.06 to 0.06
- second_moment: float32 [4, 7168, 2048], P('expert', 'dp'), may hold values from 1e-05 to 0.001
- rotation: int32 [4, 64, 1], replicated, may hold values from 0 to 63; in each aligned block of 64 rows (0 to 63, 64 to 127, ..., all dimensions but the last counted through in order) at most 3 rows name the same one
- assignment: int32 [256], replicated, may hold values from 0 to 255, each once
Outputs:
- saved_master: float32 [4, 256, 3, 448, 128], P('expert', 'dp')
- saved_update: float32 [4, 256, 3, 448, 128], P('expert', 'dp')
- checksums: float32 [4, 2, 256], replicated
Inputs may be any that keep to these rules, and one draw needn't show every extreme that they name: rotation[r, j, 0] is the dp index that writes span j of round r; within one round no index is named more than 3 times, and in some round one index is named exactly 3 times. `assignment`: a permutation of the spans' checksum slots.
All inputs are finite; a program needn't handle non-finite values.
Results may differ from a plain program's by a relative error of at most 0.00002.
Values sent between devices are 32-bit elements; how exact they have to be, the bound alone decides.
A program may use at most 64 MiB of HBM per device.

v0:
```python
import math

import jax
import jax.numpy as jnp
from jax import lax
from jax.sharding import Mesh
from jax.sharding import PartitionSpec as P

LANE = 128
MOST = 3
STEP = 20
DP = ("dp_0", "dp_1", "dp_2")
EXPERT = ("expert_0", "expert_1")
DP_EXPERT = ("dp_0", "dp_1", "dp_2", "expert_0", "expert_1")


BETA_ONE = 0.9
BETA_TWO = 0.95
EPSILON = 1e-08


def sent_together(arrays, axis, split_dim, concat_dim, along):
    ends, at = ([], 0)
    for a in arrays[:-1]:
        at += a.shape[along]
        ends.append(at)
    both = jnp.concatenate(arrays, axis=along)
    return tuple(
        jnp.split(
            lax.all_to_all(both, axis, split_axis=split_dim, concat_axis=concat_dim, tiled=True),
            ends,
            axis=along,
        )
    )


def one_axis_at_a_time(array, axes):
    for axis in axes:
        array = lax.psum(array, axis)
    return array


def scaled_moment(first_part, second_part):
    corr_one = 1.0 - BETA_ONE**STEP
    corr_two = 1.0 - BETA_TWO**STEP
    return first_part / corr_one / (jnp.sqrt(second_part / corr_two) + EPSILON)


def slot_table(rotation, dp_count, most_slots):
    owners = rotation[:, :, 0]
    span_ids = jnp.arange(dp_count, dtype=jnp.int32)
    same_writer = owners[:, :, None] == owners[:, None, :]
    before = span_ids[None, :] < span_ids[:, None]
    slot_rank = jnp.sum((same_writer & before[None]).astype(jnp.int32), axis=2)
    writers = jnp.arange(dp_count, dtype=jnp.int32)
    slot_ids = jnp.arange(most_slots, dtype=jnp.int32)
    matches = (owners[:, None, None, :] == writers[None, None, :, None]) & (
        slot_rank[:, None, None, :] == slot_ids[None, :, None, None]
    )
    matches = matches.astype(jnp.int32)
    found_any = jnp.sum(matches, axis=3)
    picked = jnp.sum(matches * span_ids, axis=3)
    return picked + (1 - found_any) * dp_count


def position_weights(line_ids, per_row, lane_count):
    row_ids = line_ids // per_row
    col_ids = line_ids % per_row * lane_count
    lane_ids = jnp.arange(lane_count, dtype=jnp.int32)
    pattern = (row_ids[..., None] * 5 + (col_ids[..., None] + lane_ids) * 3) % 11
    return 1.0 + pattern.astype(jnp.float32) / 10.0


def deliver_slots(send_parts):
    return sent_together((send_parts[0], send_parts[1]), DP, 1, 1, 0)


def shards(master, first_moment, second_moment, rotation, assignment):
    dp_count = lax.axis_size(DP)
    group_count = lax.axis_size(EXPERT)
    position = lax.axis_index(DP)
    group_id = lax.axis_index(EXPERT)
    round_count = rotation.shape[0]
    rows_here = master.shape[1]
    lane_count = LANE
    per_row = master.shape[2] // lane_count
    lines_device = rows_here * per_row
    piece_len = lines_device // (round_count * dp_count)
    inv_count = 1.0 / math.sqrt(dp_count * piece_len * lane_count)
    table = slot_table(rotation, dp_count, MOST)
    round_ids = jnp.arange(round_count, dtype=jnp.int32)[:, None, None]

    def line_pieces(field_in):
        return field_in.reshape(round_count, dp_count, piece_len, lane_count)

    def padded_pieces(line_view):
        return jnp.concatenate(
            [line_view, jnp.zeros((round_count, 1, piece_len, lane_count), line_view.dtype)], axis=1
        )

    update = scaled_moment(first_moment, second_moment)
    master_lines = line_pieces(master)
    update_lines = line_pieces(update)
    local_lines = position * lines_device + jnp.arange(lines_device, dtype=jnp.int32).reshape(
        round_count, dp_count, piece_len
    )
    weights = position_weights(local_lines, per_row, lane_count)
    master_sums = (
        jnp.sum(master_lines * weights, axis=(2, 3)).reshape(round_count * dp_count) * inv_count
    )
    update_sums = (
        jnp.sum(update_lines * weights, axis=(2, 3)).reshape(round_count * dp_count) * inv_count
    )
    sources = (padded_pieces(master_lines), padded_pieces(update_lines))
    send_parts = tuple(
        (
            source[round_ids, table].reshape(round_count * MOST, dp_count, piece_len, lane_count)
            for source in sources
        )
    )
    delivered = deliver_slots(send_parts)
    saved_master = delivered[0].reshape(round_count, MOST, dp_count, piece_len, lane_count)
    saved_update = delivered[1].reshape(round_count, MOST, dp_count, piece_len, lane_count)
    span_count = assignment.shape[0]
    slot_ids = jnp.arange(span_count, dtype=jnp.int32)
    permuting = (assignment[:, None] == slot_ids[None, :]).astype(jnp.float32)
    both_sums = jnp.stack([master_sums, update_sums])
    placed_sums = jnp.sum(both_sums[:, :, None] * permuting[None], axis=1)
    in_slot = (jnp.arange(group_count, dtype=jnp.int32) == group_id).astype(jnp.float32)
    contribution = in_slot[:, None, None] * placed_sums[None]
    checksums = one_axis_at_a_time(contribution, DP_EXPERT)
    shape_out = (1, round_count, MOST, dp_count * piece_len, lane_count)
    return (saved_master.reshape(shape_out), saved_update.reshape(shape_out), checksums)


def solution(mesh):
    torus = Mesh(
        mesh.devices.reshape(4, 4, 4, 2, 2), ("dp_0", "dp_1", "dp_2", "expert_0", "expert_1")
    )
    in_specs = (P(EXPERT, DP, None), P(EXPERT, DP, None), P(EXPERT, DP, None), P(), P())
    out_specs = (P(EXPERT, DP, None, None, None), P(EXPERT, DP, None, None, None), P())
    return jax.shard_map(
        shards, mesh=torus, in_specs=in_specs, out_specs=out_specs, check_vma=False
    )
```

profile of v0, /device:TPU:32, one launch (start us, length us, event | category | flops | bytes accessed | tf_op | source)
XLA Modules:
  0.0 216.5 jit_solution(6803758860566984017)
XLA Ops:
  0.7 0.8 iota_compare_fusion.1
  1.4 1.0 convert_reduce_fusion
  2.4 0.5 fusion.7
  3.0 0.1 reshape.229
  3.1 1.8 add_divide_fusion
  4.9 0.2 reshape.221
  5.1 1.2 reshape.219
  6.3 0.1 concatenate.15
  6.3 1.3 concatenate.13
  7.6 6.6 %gather_fusion = f32[768,7,128]{2,1,0:T(8,128)} fusion(f32[4,65,7,128]{3,2,1,0:T(8,128)S(1)} %concatenate.13, s32[768]{0:T(1024)S(1)} %reshape.229), kind=kCustom, calls=%fused_computation | custom fusion | bytes 5511168 | tf_op jit(solution)/shard_map/gather | solution.py:117
  14.3 5.3 %copy.16 = f32[12,64,7,128]{3,0,2,1:T(8,128)} copy(f32[12,64,7,128]{3,2,1,0:T(8,128)} %bitcast.12) | data formatting | bytes 5505024 | tf_op jit(solution)/shard_map/reshape | solution.py:117
  19.6 6.6 %gather_fusion.1 = f32[768,7,128]{2,1,0:T(8,128)} fusion(f32[4,65,7,128]{3,2,1,0:T(8,128)S(1)} %concatenate.15, s32[768]{0:T(1024)S(1)} %reshape.229), kind=kCustom, calls=%fused_computation.1 | custom fusion | bytes 5511168 | tf_op jit(solution)/shard_map/gather | solution.py:117
  26.2 3.7 %copy.17 = f32[12,64,7,128]{3,0,2,1:T(8,128)S(1)} copy(f32[12,64,7,128]{3,2,1,0:T(8,128)} %bitcast.11) | data formatting | bytes 5505024 | tf_op jit(solution)/shard_map/reshape | solution.py:117
  29.9 3.0 %pad_maximum_fusion = f32[24,64,7,128]{3,0,2,1:T(8,128)} fusion(f32[12,64,7,128]{3,0,2,1:T(8,128)S(1)} %copy.17, f32[12,64,7,128]{3,0,2,1:T(8,128)S(1)} %copy-done), kind=kLoop, calls=%fused_computation.2 | loop fusion | flops 1376256 | bytes 11010048 | tf_op jit(solution)/shard_map/concatenate | solution.py:27
  32.9 12.0 %all-to-all-start = ((f32[24,64,7,128]{3,0,2,1:T(8,128)}), f32[24,64,7,128]{3,0,2,1:T(8,128)}, u32[]{:S(2)}, u32[]{:S(2)}) async-start(f32[24,64,7,128]{3,0,2,1:T(8,128)} %pad_maximum_fusion), calls=%async_computation | async-start | bytes 11010048 | tf_op jit(solution)/shard_map/all_to_all | solution.py:30
  44.9 0.1 fusion.9
  45.1 7.0 %multiply_reduce_fusion.1 = (f32[4,64]{1,0:T(4,128)S(1)}, f32[4,64]{1,0:T(4,128)S(1)}) fusion(f32[4,64,7,128]{3,2,1,0:T(8,128)S(1)} %copy-done.1, s32[4,64,7]{2,1,0:T(8,128)S(1)} %get-tuple-element.10, s32[4,64,7]{2,1,0:T(8,128)S(1)} %get-tuple-element.9, f32[4,64,7,128]{3,2,1,0:T(8,128)S(1)} %reshape.221), kind=kLoop, calls=%fused_computation.8 | loop fusion | flops 3669504 | bytes 1851392 | tf_op jit(solution)/shard_map/reduce_sum | solution.py:109
  52.0 0.1 mul.152
  52.1 0.1 mul.155
  52.2 0.1 fusion.8
  52.3 0.1 multiply_reduce_fusion.2
  52.5 0.1 broadcast_multiply_fusion
  52.6 34.0 %psum.35 = f32[4,2,256]{2,1,0:T(2,128)S(1)} all-reduce(f32[4,2,256]{2,1,0:T(2,128)S(1)} %broadcast_multiply_fusion), channel_id=1, replica_groups=mesh['dp_0'=4,'dp_1'=4,'dp_2'=4,'expert_0'=2,'expert_1'=2] {'dp_0'}, use_global_device_ids=true, to_apply=%region_6.7 | all-reduce | flops 2048 | bytes 16384 | tf_op jit(solution)/shard_map/psum | solution.py:39
  86.5 79.6 %psum.36 = f32[4,2,256]{2,1,0:T(2,128)S(1)} all-reduce(f32[4,2,256]{2,1,0:T(2,128)S(1)} %psum.35), channel_id=1, replica_groups=mesh['dp_0'=4,'dp_1'=4,'dp_2'=4,'expert_0'=2,'expert_1'=2] {'dp_1'}, use_global_device_ids=true, to_apply=%region_7.8 | all-reduce | flops 2048 | bytes 16384 | tf_op jit(solution)/shard_map/psum | solution.py:39
  166.1 10.5 %psum.37 = f32[4,2,256]{2,1,0:T(2,128)S(1)} all-reduce(f32[4,2,256]{2,1,0:T(2,128)S(1)} %psum.36), channel_id=1, replica_groups=mesh['dp_0'=4,'dp_1'=4,'dp_2'=4,'expert_0'=2,'expert_1'=2] {'dp_2'}, use_global_device_ids=true, to_apply=%region_8.9 | all-reduce | flops 2048 | bytes 16384 | tf_op jit(solution)/shard_map/psum | solution.py:39
  176.6 8.9 %psum.38 = f32[4,2,256]{2,1,0:T(2,128)S(1)} all-reduce(f32[4,2,256]{2,1,0:T(2,128)S(1)} %psum.37), channel_id=1, replica_groups=mesh['dp_0'=4,'dp_1'=4,'dp_2'=4,'expert_0'=2,'expert_1'=2] {'expert_0'}, use_global_device_ids=true, to_apply=%region_9.10 | all-reduce | flops 2048 | bytes 16384 | tf_op jit(solution)/shard_map/psum | solution.py:39
  185.5 3.2 %psum.39 = f32[4,2,256]{2,1,0:T(2,128)} all-reduce(f32[4,2,256]{2,1,0:T(2,128)S(1)} %psum.38), channel_id=1, replica_groups=mesh['dp_0'=4,'dp_1'=4,'dp_2'=4,'expert_0'=2,'expert_1'=2] {'expert_1'}, use_global_device_ids=true, to_apply=%region_10.11 | all-reduce | flops 2048 | bytes 16384 | tf_op jit(solution)/shard_map/psum | solution.py:39
  188.8 6.8 %fusion.17 = (f32[12,64,7,128]{3,0,2,1:T(8,128)}, f32[12,64,7,128]{3,0,2,1:T(8,128)}) fusion(f32[24,64,7,128]{3,0,2,1:T(8,128)} %all-to-all-done), kind=kLoop, calls=%fused_computation.47 | loop fusion | bytes 11010048 | tf_op jit(solution)/shard_map/split | solution.py:29
  195.6 6.0 %reshape.244 = f32[1,4,3,448,128]{4,2,1,3,0:T(4,128)} reshape(f32[12,64,7,128]{3,0,2,1:T(8,128)} %get-tuple-element.7) | data formatting | bytes 5505024 | tf_op jit(solution)/shard_map/reshape;reshape | solution.py:133
  201.6 4.5 %copy.21 = f32[1,4,3,448,128]{4,3,2,1,0:T(8,128)} copy(f32[1,4,3,448,128]{4,2,1,3,0:T(4,128)} %reshape.244) | data formatting | bytes 5505024 | tf_op jit(solution)/shard_map/reshape;reshape | solution.py:133
  206.0 6.0 %reshape.243 = f32[1,4,3,448,128]{4,2,1,3,0:T(4,128)} reshape(f32[12,64,7,128]{3,0,2,1:T(8,128)} %get-tuple-element.8) | data formatting | bytes 5505024 | tf_op jit(solution)/shard_map/reshape;reshape | solution.py:133
  212.1 4.5 %copy.20 = f32[1,4,3,448,128]{4,3,2,1,0:T(8,128)} copy(f32[1,4,3,448,128]{4,2,1,3,0:T(4,128)} %reshape.243) | data formatting | bytes 5505024 | tf_op jit(solution)/shard_map/reshape;reshape | solution.py:133
  (18 shorter events, 0.1 us)
Async XLA Ops:
  0.6 4.5 %copy-start.2 = (f32[1,112,2048]{2,1,0:T(8,128)S(1)}, f32[1,112,2048]{2,1,0:T(8,128)}, u32[]{:S(2)}) copy-start(f32[1,112,2048]{2,1,0:T(8,128)} %param.5) | copy-start | bytes 2752516
  26.2 3.7 %copy-start = (f32[12,64,7,128]{3,0,2,1:T(8,128)S(1)}, f32[12,64,7,128]{3,0,2,1:T(8,128)}, u32[]{:S(2)}) copy-start(f32[12,64,7,128]{3,0,2,1:T(8,128)} %copy.16) | copy-start | bytes 8257540
  32.9 12.1 %copy-start.1 = (f32[4,64,7,128]{3,2,1,0:T(8,128)S(1)}, f32[4,64,7,128]{3,2,1,0:T(8,128)}, u32[]{:S(2)}) copy-start(f32[4,64,7,128]{3,2,1,0:T(8,128)} %reshape.219) | copy-start | bytes 2752516
  32.9 19.3 %copy-start.3 = (s32[256]{0:T(256)S(1)}, s32[256]{0:T(256)}, u32[]{:S(2)}) copy-start(s32[256]{0:T(256)} %param.9) | copy-start | bytes 3076
  32.9 155.8 %all-to-all-start = ((f32[24,64,7,128]{3,0,2,1:T(8,128)}), f32[24,64,7,128]{3,0,2,1:T(8,128)}, u32[]{:S(2)}, u32[]{:S(2)}) async-start(f32[24,64,7,128]{3,0,2,1:T(8,128)} %pad_maximum_fusion), calls=%async_computation | async-start | bytes 11010048 | tf_op jit(solution)/shard_map/all_to_all | solution.py:30
where the time goes:
time: 218 us; the launch traced here: 217 us
  blocking collectives  136 us (62%)
  local copies, waits for them, and re-layouts  53 us (24%)
  other arithmetic  14.6 us (7%)
  starting transfers between devices  12 us (6%)
    psum x5, blocking collectives, one_axis_at_a_time(): array = lax.psum(array, axis)  136 us
    gather x2, local copies, waits for them, and re-layouts, shards(): source[round_ids, table]  13.2 us
    all_to_all x1, starting transfers between devices, sent_together(): lax.all_to_all(both, axis, split_axis=split_dim, concat_axis=concat_dim,...  12 us
    another operation x2, local copies, waits for them, and re-layouts, shards(): saved_update.reshape(shape_out)  10.5 us
    another operation x2, local copies, waits for them, and re-layouts, shards(): saved_master.reshape(shape_out)  10.5 us
    reshape x2, local copies, waits for them, and re-layouts, shards(): source[round_ids, table]  9.03 us
    reduce_sum x1, other arithmetic, shards(): jnp.sum(master_lines * weights, axis=(2, 3)).reshape(round_count * dp_count)  6.96 us
    split x1, local copies, waits for them, and re-layouts, sent_together(): jnp.split(lax.all_to_all(both, axis, split_axis=split_dim, concat_axis=co...  6.82 us
  transfers between devices with their start and end apart: 1, of which 0 were waited for; matrix products, arithmetic and copies ran while one was open for 4% of the time, Pallas kernels for 0%

commit v1 on v0

v1 whole, which is shorter than its diff:
```python
import functools
import math

import jax
import jax.numpy as jnp
from jax import lax
from jax.experimental import pallas as pl
from jax.experimental.pallas import tpu as pltpu
from jax.sharding import Mesh
from jax.sharding import PartitionSpec as P

LANE = 128
MOST = 3
STEP = 20
BETA_ONE = 0.9
BETA_TWO = 0.95
EPSILON = 1e-08
DP = ("dp_0", "dp_1", "dp_2")
EXPERT = ("expert_0", "expert_1")
MESH = pl.DeviceIdType.MESH

N = 4
ROUNDS = 4
SPANS = 256
PIECE = 7
SLOTS = ROUNDS * MOST
BLOCK = N * SLOTS
PLANE = N * N
USUAL = 96
ALL = PLANE * SLOTS


def three_parts(x):
    hi = x.astype(jnp.bfloat16)
    rest = x - hi.astype(jnp.float32)
    mid = rest.astype(jnp.bfloat16)
    low = (rest - mid.astype(jnp.float32)).astype(jnp.bfloat16)
    return hi, mid, low


def select_rows(choice, x):
    hi, mid, low = (
        jnp.dot(choice, part, preferred_element_type=jnp.float32) for part in three_parts(x)
    )
    return hi + mid + low


def prepare(room, master, first, second, rot_row, rot_col, packed, sums, target, lin_m, lin_u):
    x, z, y = (lax.axis_index(axis) for axis in DP)
    position = (x * N + z) * N + y
    corr_one = 1.0 - BETA_ONE**STEP
    corr_two = 1.0 - BETA_TWO**STEP
    per_row = master.shape[1] // LANE
    rows = master.shape[0]
    for col in range(per_row):
        at = slice(col * LANE, (col + 1) * LANE)
        lin_m[pl.ds(col, rows, stride=per_row), :] = master[:, at]
        lin_u[pl.ds(col, rows, stride=per_row), :] = (first[:, at] / corr_one) / (
            jnp.sqrt(second[:, at] / corr_two) + EPSILON
        )

    row_id = lax.broadcasted_iota(jnp.int32, (SPANS, SPANS), 0)
    col_id = lax.broadcasted_iota(jnp.int32, (SPANS, SPANS), 1)
    w_row, w_col = rot_row[...], rot_col[...]
    z_row, z_col = (w_row // N) % N, (w_col // N) % N
    same_z = z_col == z_row
    place_row = jnp.sum(jnp.where(same_z & (row_id < col_id), 1, 0), axis=0, keepdims=True)
    place_col = jnp.sum(jnp.where(same_z & (col_id < row_id), 1, 0), axis=1, keepdims=True)
    same_w = (w_col == w_row) & (row_id // (N * PLANE) == col_id // (N * PLANE))
    slot_col = jnp.sum(jnp.where(same_w & (col_id < row_id), 1, 0), axis=1, keepdims=True)

    lines = lax.broadcasted_iota(jnp.int32, (N * room, SPANS), 0)
    choice = (lines == z_row * room + place_row).astype(jnp.float32).astype(jnp.bfloat16)

    round_col = lax.broadcasted_iota(jnp.int32, (SPANS, 1), 0) // (N * PLANE)
    writer_col = (w_col // PLANE) * N + w_col % N
    value_col = writer_col * (2 * SLOTS) + round_col * MOST + slot_col
    lane = lax.broadcasted_iota(jnp.int32, (SPANS, 2 * room), 1)
    second_half = lane >= room
    here = (z_col == z) & (place_col == jnp.where(second_half, lane - room, lane))
    value = value_col + jnp.where(second_half, SLOTS, 0)
    found = jnp.sum(jnp.where(here, value + 1, 0), axis=0, keepdims=True) - 1
    target[...] = jnp.broadcast_to(found, target.shape)

    total_m = jnp.zeros((SPANS, LANE), jnp.float32)
    total_u = jnp.zeros((SPANS, LANE), jnp.float32)
    span = lax.broadcasted_iota(jnp.int32, (SPANS, LANE), 0)
    entry = lax.broadcasted_iota(jnp.int32, (SPANS, LANE), 1)
    shift = (5 * rows * position) % 11
    for part in range(PIECE):
        x_m = lin_m[pl.ds(part, SPANS, stride=PIECE), :]
        x_u = lin_u[pl.ds(part, SPANS, stride=PIECE), :]
        line = span * PIECE + part
        number = 5 * (line // per_row) + 3 * ((line % per_row) * LANE + entry) + shift
        number = number.astype(jnp.float32)
        pattern = number - 11.0 * jnp.floor((number + 0.5) * (1.0 / 11.0))
        weight = 1.0 + pattern * 0.1
        total_m += x_m * weight
        total_u += x_u * weight
        packed[part] = select_rows(choice, jnp.concatenate([x_m, x_u], axis=1))

    scale = 1.0 / math.sqrt(N * PLANE * PIECE * LANE)
    ones = jnp.ones((8, LANE), jnp.float32)
    sums[...] = jnp.zeros_like(sums)
    for i, total in enumerate((total_m, total_u)):
        row = scale * lax.dot_general(
            ones,
            total,
            (((1,), (1,)), ((), ())),
            precision=lax.Precision.HIGHEST,
            preferred_element_type=jnp.float32,
        )
        for half in range(2):
            sums[2 * i + half : 2 * i + half + 1, :] = row[0:1, half * LANE : (half + 1) * LANE]


def exchange(
    room,
    packed,
    sums,
    target,
    out,
    sums_out,
    near,
    ready,
    sums_z,
    sums_p,
    sums_e,
    line_sum,
    plane_sum,
    own_sem,
    keep_sem,
    z_send,
    z_recv,
    p_send,
    p_recv,
    s_send,
    s_recv,
):
    x, z, y = (lax.axis_index(axis) for axis in DP)
    e_0, e_1 = (lax.axis_index(axis) for axis in EXPERT)
    here = x * N + y

    def on_line(step):
        return lax.rem(z + step, N)

    def in_plane(step):
        return lax.rem(x + step // N, N), lax.rem(y + step % N, N)

    def line_id(step):
        return {"dp_1": on_line(step)}

    def plane_id(step):
        to_x, to_y = in_plane(step)
        return {"dp_0": to_x, "dp_2": to_y}

    def expert_id(step):
        return {"expert_0": lax.rem(e_0 + step // 2, 2), "expert_1": lax.rem(e_1 + step % 2, 2)}

    barrier = pltpu.get_barrier_semaphore()
    others = [line_id(s) for s in range(1, N)]
    others += [plane_id(s) for s in range(1, PLANE)]
    others += [expert_id(s) for s in range(1, N)]
    for other in others:
        pl.semaphore_signal(barrier, inc=1, device_id=other, device_id_type=MESH)
    pl.semaphore_wait(barrier, len(others))

    def send(src, dst, send_sem, recv_sem, device):
        copy = pltpu.make_async_remote_copy(
            src_ref=src,
            dst_ref=dst,
            send_sem=send_sem,
            recv_sem=recv_sem,
            device_id=device,
            device_id_type=MESH,
        )
        copy.start()
        return copy

    sum_line = [
        send(sums, sums_z.at[z], s_send.at[s - 1], s_recv.at[s - 1], line_id(s))
        for s in range(1, N)
    ]
    sums_z[z] = sums[...]

    mine = pl.ds(pl.multiple_of(z * room, 8), room)
    lines = []
    for part in range(PIECE):
        for s in (2, 1, 3):
            theirs = pl.ds(pl.multiple_of(on_line(s) * room, 8), room)
            lines.append(
                send(
                    packed.at[part, theirs],
                    near.at[part, mine],
                    z_send.at[part, s - 1],
                    z_recv.at[part, s - 1],
                    line_id(s),
                )
            )
    owns = []
    for part in range(PIECE):
        own = pltpu.make_async_copy(packed.at[part, mine], near.at[part, mine], own_sem.at[part])
        own.start()
        owns.append(own)

    wide = lax.broadcasted_iota(jnp.int32, (2 * BLOCK // 4 * PLANE, 2 * room), 0)
    choice = (wide == target[0:1, :]).astype(jnp.float32).astype(jnp.bfloat16)
    home = pl.ds(pl.multiple_of(here * BLOCK, 8), BLOCK)
    planes, sum_plane, sum_expert = [], [], []
    for part in range(PIECE):
        owns[part].wait()
        for copy in lines[3 * part : 3 * part + 3]:
            copy.wait_recv()
        if part == 0:
            for copy in sum_line:
                copy.wait_recv()
            line_sum[...] = sums_z[0] + sums_z[1] + sums_z[2] + sums_z[3]
            sums_p[here] = line_sum[...]
            for s in range(1, PLANE):
                at = N - 2 + s
                sum_plane.append(
                    send(line_sum, sums_p.at[here], s_send.at[at], s_recv.at[at], plane_id(s))
                )
        if part == 2:
            for copy in sum_plane:
                copy.wait_recv()
            total = sums_p[0]
            for d in range(1, PLANE):
                total = total + sums_p[d]
            plane_sum[...] = total
            sums_e[e_0 * 2 + e_1] = total
            for s in range(1, N):
                at = N + PLANE - 3 + s
                sum_expert.append(
                    send(
                        plane_sum,
                        sums_e.at[e_0 * 2 + e_1],
                        s_send.at[at],
                        s_recv.at[at],
                        expert_id(s),
                    )
                )
        for half in range(2):
            got = select_rows(choice, near[part, 2 * room * half : 2 * room * (half + 1), :])
            rows = slice(2 * SLOTS * half, 2 * SLOTS * (half + 1))
            for t in range(2):
                ready[part, :, t, rows, :] = got[:, t * LANE : (t + 1) * LANE].reshape(
                    PLANE, 2 * SLOTS, LANE
                )
        for i in range(1, PLANE):
            s = 1 + (i - 1 + 2 * part) % (PLANE - 1)
            to_x, to_y = in_plane(s)
            planes.append(
                send(
                    ready.at[part, to_x * N + to_y],
                    out.at[part, :, home],
                    p_send.at[part, s - 1],
                    p_recv.at[part, s - 1],
                    plane_id(s),
                )
            )
        keep = pltpu.make_async_copy(ready.at[part, here], out.at[part, :, home], keep_sem.at[part])
        keep.start()
        owns.append(keep)

    for copy in sum_expert:
        copy.wait_recv()
    sums_out[...] = sums_e[...]
    for copy in owns[PIECE:]:
        copy.wait()
    for copy in lines + sum_line + sum_plane + sum_expert:
        copy.wait_send()
    for copy in planes:
        copy.wait()


def unpack(got, sums, file_slot, saved_m, saved_u, checks, lines, full_m, full_u, both, in_sem, out_sem):
    copies = []
    for part in range(PIECE):
        copy = pltpu.make_async_copy(got.at[part], lines.at[part], in_sem.at[part])
        copy.start()
        copies.append(copy)

    for g in range(N):
        for i in range(2):
            for half in range(2):
                both[2 * g + i : 2 * g + i + 1, half * LANE : (half + 1) * LANE] = sums[
                    g, 2 * i + half : 2 * i + half + 1, :
                ]
    lane = lax.broadcasted_iota(jnp.int32, (SPANS, SPANS), 1)
    placing = (file_slot[...] == lane).astype(jnp.float32)
    checks[...] = jnp.dot(
        both[...],
        placing,
        precision=lax.Precision.HIGHEST,
        preferred_element_type=jnp.float32,
    )

    for part in range(PIECE):
        copies[part].wait()

        def one_slot(slot, _, part=part):
            for t, full in enumerate((full_m, full_u)):
                for to_x in range(N):
                    for to_z in range(N):
                        rows = lines[
                            part, t, pl.ds(to_x * N * BLOCK + to_z * SLOTS + slot, N, stride=BLOCK), :
                        ]
                        first = (to_x * PLANE + to_z * N) * PIECE + part
                        full[slot, pl.ds(first, N, stride=PIECE), :] = rows
            return _

        lax.fori_loop(0, SLOTS, one_slot, 0)
    outs = [
        pltpu.make_async_copy(full_m, saved_m, out_sem.at[0]),
        pltpu.make_async_copy(full_u, saved_u, out_sem.at[1]),
    ]
    for copy in outs:
        copy.start()
    for copy in outs:
        copy.wait()


VMEM = pl.BlockSpec(memory_space=pltpu.VMEM)
ANY = pl.BlockSpec(memory_space=pl.ANY)
F32 = jnp.float32


def move(room, number, master, first, second, rot_row, rot_col):
    lines = master.shape[0] * master.shape[1] // LANE
    packed, sums, target = pl.pallas_call(
        functools.partial(prepare, room),
        out_shape=(
            jax.ShapeDtypeStruct((PIECE, N * room, 2 * LANE), F32),
            jax.ShapeDtypeStruct((8, LANE), F32),
            jax.ShapeDtypeStruct((8, 2 * room), jnp.int32),
        ),
        in_specs=[VMEM] * 5,
        out_specs=(VMEM, VMEM, VMEM),
        scratch_shapes=[pltpu.VMEM((lines, LANE), F32), pltpu.VMEM((lines, LANE), F32)],
    )(master, first, second, rot_row, rot_col)
    small = 2 * (N - 1) + PLANE - 1
    return pl.pallas_call(
        functools.partial(exchange, room),
        out_shape=(
            jax.ShapeDtypeStruct((PIECE, 2, PLANE * BLOCK, LANE), F32),
            jax.ShapeDtypeStruct((N, 8, LANE), F32),
        ),
        in_specs=[VMEM] * 3,
        out_specs=(ANY, VMEM),
        scratch_shapes=[
            pltpu.VMEM((PIECE, N * room, 2 * LANE), F32),
            pltpu.VMEM((PIECE, PLANE, 2, BLOCK, LANE), F32),
            pltpu.VMEM((N, 8, LANE), F32),
            pltpu.VMEM((PLANE, 8, LANE), F32),
            pltpu.VMEM((N, 8, LANE), F32),
            pltpu.VMEM((8, LANE), F32),
            pltpu.VMEM((8, LANE), F32),
            pltpu.SemaphoreType.DMA((PIECE,)),
            pltpu.SemaphoreType.DMA((PIECE,)),
            pltpu.SemaphoreType.DMA((PIECE, N - 1)),
            pltpu.SemaphoreType.DMA((PIECE, N - 1)),
            pltpu.SemaphoreType.DMA((PIECE, PLANE - 1)),
            pltpu.SemaphoreType.DMA((PIECE, PLANE - 1)),
            pltpu.SemaphoreType.DMA((small,)),
            pltpu.SemaphoreType.DMA((small,)),
        ],
        compiler_params=pltpu.CompilerParams(collective_id=number, has_side_effects=True),
    )(packed, sums, target)


def shards(master, first, second, rotation, assignment):
    owners = rotation.reshape(1, SPANS)
    planes = jnp.arange(N, dtype=jnp.int32)[:, None]
    load = jnp.sum(((owners // N) % N == planes).astype(jnp.int32), axis=1)
    got, sums = lax.cond(
        jnp.max(load) <= USUAL,
        functools.partial(move, USUAL, 0),
        functools.partial(move, ALL, 1),
        master[0],
        first[0],
        second[0],
        owners,
        rotation.reshape(SPANS, 1),
    )
    length = N * PLANE * PIECE
    saved_m, saved_u, checks = pl.pallas_call(
        unpack,
        out_shape=(
            jax.ShapeDtypeStruct((SLOTS, length, LANE), F32),
            jax.ShapeDtypeStruct((SLOTS, length, LANE), F32),
            jax.ShapeDtypeStruct((2 * N, SPANS), F32),
        ),
        in_specs=[ANY, VMEM, VMEM],
        out_specs=(ANY, ANY, VMEM),
        scratch_shapes=[
            pltpu.VMEM((PIECE, 2, PLANE * BLOCK, LANE), F32),
            pltpu.VMEM((SLOTS, length, LANE), F32),
            pltpu.VMEM((SLOTS, length, LANE), F32),
            pltpu.VMEM((2 * N, SPANS), F32),
            pltpu.SemaphoreType.DMA((PIECE,)),
            pltpu.SemaphoreType.DMA((2,)),
        ],
    )(got, sums, assignment.reshape(SPANS, 1))
    shape = (1, ROUNDS, MOST, length, LANE)
    return saved_m.reshape(shape), saved_u.reshape(shape), checks.reshape(N, 2, SPANS)


def solution(mesh):
    torus = Mesh(mesh.devices.reshape(N, N, N, 2, 2), DP + EXPERT)
    rows = P(EXPERT, DP, None)
    saved = P(EXPERT, DP, None, None, None)
    return jax.shard_map(
        shards,
        mesh=torus,
        in_specs=(rows, rows, rows, P(), P()),
        out_specs=(saved, saved, P()),
        check_vma=False,
    )
```

time: 218 us -> 124 us (0.57)
  blocking collectives: 136 us -> 0 us
  Pallas kernels: 0 us -> 116 us
  local copies, waits for them, and re-layouts: 53 us -> 5.01 us
  other arithmetic: 14.6 us -> 2.12 us
  starting transfers between devices: 12 us -> 0 us
    psum x5 -> x0, blocking collectives: 136 us -> none  [one_axis_at_a_time(): array = lax.psum(array, axis)]
    pallas_call x0 -> x3, Pallas kernels: none -> 116 us  [the longest x1 101 us: move(): pl.pallas_call(functools.partial(exchange, room), out_shape=(jax.ShapeDty...]
    another operation x4 -> x1, local copies, waits for them, and re-layouts: 20.9 us -> 0.8 us  [the longest x2 10.5 us: shards(): saved_update.reshape(shape_out)]
    gather x2 -> x0, local copies, waits for them, and re-layouts: 13.2 us -> none  [shards(): source[round_ids, table]]
    all_to_all x1 -> x0, starting transfers between devices: 12 us -> none  [sent_together(): lax.all_to_all(both, axis, split_axis=split_dim, concat_axis=concat_dim,...]
    reduce_sum x4 -> x1, other arithmetic: 8.59 us -> 0.12 us  [shards(): load = jnp.sum((owners // N % N == planes).astype(jnp.int32), axis=1)]
    split x1 -> x0, local copies, waits for them, and re-layouts: 6.82 us -> none  [sent_together(): jnp.split(lax.all_to_all(both, axis, split_axis=split_dim, concat_axis=co...]
    reshape x4 -> x5, local copies, waits for them, and re-layouts: 10.4 us -> 3.7 us  [the longest x1 1.3 us: shards(): checks.reshape(N, 2, SPANS)]
  transfers between devices with their start and end apart: 1 -> 0, of which waited for: 0 -> 0; matrix products, arithmetic and copies ran while one was open for 4% -> 0% of each run, Pallas kernels for 0% -> 0%
where the time goes in v1:
time: 124 us
  Pallas kernels  116 us (94%)
  local copies, waits for them, and re-layouts  5.01 us (4%)
  other arithmetic  2.12 us (2%)
  between operations  1.32 us (1%)
    pallas_call x1, Pallas kernels, move(): pl.pallas_call(functools.partial(exchange, room), out_shape=(jax.ShapeDty...  101 us
    pallas_call x1, Pallas kernels, shards(): pl.pallas_call(unpack, out_shape=(jax.ShapeDtypeStruct((SLOTS, length, LA...  7.68 us
    pallas_call x1, Pallas kernels, move(): pl.pallas_call(functools.partial(prepare, room), out_shape=(jax.ShapeDtyp...  6.76 us

profile of v1, /device:TPU:32, one launch (start us, length us, event | category | flops | bytes accessed | tf_op | source)
XLA Modules:
  0.0 124.2 jit_solution(14730186657734472649)
XLA Ops:
  0.6 0.8 reshape.103
  1.4 0.8 reshape.104
  2.2 0.5 broadcast.75
  2.7 1.3 %reduce.7 = s32[4,64]{1,0:T(4,128)S(1)} reduce(s32[4,64,1]{1,2,0:T(1,128)} %param.10, s32[]{:T(128)} %broadcast.75), dimensions={2}, to_apply=%param.10.reduce_sub_computation.7 | reduce | bytes 2052 | tf_op args[3]
  4.0 0.1 reshape.102
  4.1 0.1 convert_reduce_fusion
  4.2 0.6 reduce_max.9
  5.5 0.0 copy-start
  5.5 108.8 %conditional.1 = ((f32[7,2,768,128]{3,2,1,0:T(8,128)}, f32[4,8,128]{2,1,0:T(8,128)S(1)})) conditional(s32[]{:T(128)} %convert_element_type.7, (f32[112,2048]{1,0:T(8,128)}, f32[112,2048]{1,0:T(8,128)}, f32[112,2048]{1,0:T(8,128)}, s32[1,256]{1,0:T(1,128)S(1)}, s32[256,1]{0,1:T(1,128)S(1)}) %tuple.28, (f32[112,2048]{1,0:T(8,128)}, ...), branch_computations={%region_2.3_spmd, %region_3.4_spmd} | conditional | bytes 2056 | solution.py:376
  5.7 0.8 copy.12.rot_col
  6.5 6.8 %branch_1_fun.2 = (f32[7,384,256]{2,1,0:T(8,128)}, f32[8,128]{1,0:T(8,128)}, s32[8,192]{1,0:T(8,128)}) custom-call(f32[112,2048]{1,0:T(8,128)} %get-tuple-element.28.master, f32[112,2048]{1,0:T(8,128)} %get-tuple-element.29.first, f32[112,2048]{1,0:T(8,128)} %get-tuple-element.30.second, s32[1,256]{1,0:T(1,128)S(1)} %get-tuple-element.31.rot_row, ...), custom_call_target="tpu_custom_call" | custom-call | tf_op jit(solution)/shard_map/cond/branch_1_fun/pallas_call | solution.py:331
  13.3 101.1 %branch_1_fun.3 = (f32[7,2,768,128]{3,2,1,0:T(8,128)}, f32[4,8,128]{2,1,0:T(8,128)S(1)}) custom-call(f32[7,384,256]{2,1,0:T(8,128)} %get-tuple-element.33.packed, f32[8,128]{1,0:T(8,128)} %get-tuple-element.34.sums, s32[8,192]{1,0:T(8,128)} %get-tuple-element.35.target), custom_call_target="tpu_custom_call" | custom-call | tf_op jit(solution)/shard_map/cond/branch_1_fun/pallas_call | solution.py:343
  114.4 0.0 copy-done
  114.4 0.8 copy.13.file_slot
  115.2 7.7 %shard_map.76 = (f32[12,448,128]{2,1,0:T(8,128)}, f32[12,448,128]{2,1,0:T(8,128)}, f32[8,256]{1,0:T(8,128)}) custom-call(f32[7,2,768,128]{3,2,1,0:T(8,128)} %get-tuple-element.44.got, f32[4,8,128]{2,1,0:T(8,128)S(1)} %get-tuple-element.45.sums, s32[256,1]{1,0:T(8,128)} %copy.13.file_slot), custom_call_target="tpu_custom_call" | custom-call | tf_op jit(solution)/shard_map/pallas_call | solution.py:387
  122.9 1.3 %reshape.108 = f32[4,2,256]{2,1,0:T(2,128)} reshape(f32[8,256]{1,0:T(8,128)} %get-tuple-element.48) | data formatting | bytes 16384 | tf_op jit(solution)/shard_map/reshape | solution.py:406
  (1 shorter events, 0.0 us)
Async XLA Ops:
  5.5 108.8 %copy-start = (s32[256]{0:T(256)S(1)}, s32[256]{0:T(256)}, u32[]{:S(2)}) copy-start(s32[256]{0:T(256)} %param.11) | copy-start | bytes 3076

commit v2 on v1

v2 whole, which is shorter than its diff:
```python
import functools
import math

import jax
import jax.numpy as jnp
from jax import lax
from jax.experimental import pallas as pl
from jax.experimental.pallas import tpu as pltpu
from jax.sharding import Mesh
from jax.sharding import PartitionSpec as P

LANE = 128
MOST = 3
STEP = 20
BETA_ONE = 0.9
BETA_TWO = 0.95
EPSILON = 1e-08
DP = ("dp_0", "dp_1", "dp_2")
EXPERT = ("expert_0", "expert_1")
MESH = pl.DeviceIdType.MESH

N = 4
ROUNDS = 4
SPANS = 256
PIECE = 7
SLOTS = ROUNDS * MOST
BLOCK = N * SLOTS
PLANE = N * N
USUAL = 96
PARTS = 2 * PIECE
AHEAD = 2
ALL = PLANE * SLOTS


def three_parts(x):
    hi = x.astype(jnp.bfloat16)
    rest = x - hi.astype(jnp.float32)
    mid = rest.astype(jnp.bfloat16)
    low = (rest - mid.astype(jnp.float32)).astype(jnp.bfloat16)
    return hi, mid, low


def select_rows(choice, x):
    parts = jnp.concatenate(three_parts(x), axis=1)
    got = jnp.dot(choice, parts, preferred_element_type=jnp.float32)
    width = x.shape[1]
    return got[:, :width] + got[:, width : 2 * width] + got[:, 2 * width :]


def flat_row(rotation, flat):
    width = rotation.shape[1]
    for r in range(ROUNDS):
        flat[0:1, r * width : (r + 1) * width] = rotation[r : r + 1, :]
    return flat[0:1, :]


def plane_load(rotation, fits):
    plane = (rotation[...] // N) % N
    load = [jnp.sum(jnp.where(plane == k, 1.0, 0.0)) for k in range(N)]
    most = functools.reduce(jnp.maximum, load)
    fits[0] = (most <= USUAL).astype(jnp.int32)


def exchange(
    room,
    master,
    first,
    second,
    rotation,
    out,
    sums_out,
    in_m,
    in_one,
    in_two,
    flat,
    lin_m,
    lin_u,
    packed,
    near,
    ready,
    sums,
    sums_z,
    sums_p,
    sums_e,
    line_sum,
    plane_sum,
    in_sem,
    own_sem,
    keep_sem,
    z_send,
    z_recv,
    p_send,
    p_recv,
    s_send,
    s_recv,
):
    x, z, y = (lax.axis_index(axis) for axis in DP)
    e_0, e_1 = (lax.axis_index(axis) for axis in EXPERT)
    here = x * N + y

    loads = []
    for i, (src, dst) in enumerate(((master, in_m), (first, in_one), (second, in_two))):
        load = pltpu.make_async_copy(src, dst, in_sem.at[i])
        load.start()
        loads.append(load)

    def on_line(step):
        return lax.rem(z + step, N)

    def in_plane(step):
        return lax.rem(x + step // N, N), lax.rem(y + step % N, N)

    def line_id(step):
        return {"dp_1": on_line(step)}

    def plane_id(step):
        to_x, to_y = in_plane(step)
        return {"dp_0": to_x, "dp_2": to_y}

    def expert_id(step):
        return {"expert_0": lax.rem(e_0 + step // 2, 2), "expert_1": lax.rem(e_1 + step % 2, 2)}

    barrier = pltpu.get_barrier_semaphore()
    others = [line_id(s) for s in range(1, N)]
    others += [plane_id(s) for s in range(1, PLANE)]
    others += [expert_id(s) for s in range(1, N)]
    for other in others:
        pl.semaphore_signal(barrier, inc=1, device_id=other, device_id_type=MESH)

    def send(src, dst, send_sem, recv_sem, device):
        copy = pltpu.make_async_remote_copy(
            src_ref=src,
            dst_ref=dst,
            send_sem=send_sem,
            recv_sem=recv_sem,
            device_id=device,
            device_id_type=MESH,
        )
        copy.start()
        return copy

    row_id = lax.broadcasted_iota(jnp.int32, (SPANS, SPANS), 0)
    col_id = lax.broadcasted_iota(jnp.int32, (SPANS, SPANS), 1)
    w_row = flat_row(rotation, flat)
    w_col = jnp.sum(jnp.where(row_id == col_id, w_row, 0), axis=1, keepdims=True)
    z_row, z_col = (w_row // N) % N, (w_col // N) % N
    same_z = z_col == z_row
    place_row = jnp.sum(jnp.where(same_z & (row_id < col_id), 1, 0), axis=0, keepdims=True)
    lines_id = lax.broadcasted_iota(jnp.int32, (N * room, SPANS), 0)
    by_plane = (lines_id == z_row * room + place_row).astype(jnp.float32).astype(jnp.bfloat16)

    rows, per_row = in_m.shape[0], in_m.shape[1] // LANE
    loads[0].wait()
    for col in range(per_row):
        at = slice(col * LANE, (col + 1) * LANE)
        lin_m[pl.ds(col, rows, stride=per_row), :] = in_m[:, at]

    def piece_lines(part):
        source = (lin_m, lin_u)[part // PIECE]
        return source[pl.ds(part % PIECE, SPANS, stride=PIECE), :]

    mine = pl.ds(pl.multiple_of(z * room, 8), room)
    lines, owns = [], []

    def pack(part):
        packed[part] = select_rows(by_plane, piece_lines(part))

    def send_line(part):
        for s in (2, 1, 3):
            theirs = pl.ds(pl.multiple_of(on_line(s) * room, 8), room)
            lines.append(
                send(
                    packed.at[part, theirs],
                    near.at[part, mine],
                    z_send.at[part, s - 1],
                    z_recv.at[part, s - 1],
                    line_id(s),
                )
            )
        own = pltpu.make_async_copy(packed.at[part, mine], near.at[part, mine], own_sem.at[part])
        own.start()
        owns.append(own)

    pack(0)
    pl.semaphore_wait(barrier, len(others))
    send_line(0)
    for part in range(1, AHEAD):
        pack(part)
        send_line(part)

    corr_one = 1.0 - BETA_ONE**STEP
    corr_two = 1.0 - BETA_TWO**STEP
    loads[1].wait()
    loads[2].wait()
    for col in range(per_row):
        at = slice(col * LANE, (col + 1) * LANE)
        lin_u[pl.ds(col, rows, stride=per_row), :] = (in_one[:, at] / corr_one) / (
            jnp.sqrt(in_two[:, at] / corr_two) + EPSILON
        )
    totals = [jnp.zeros((SPANS, LANE), jnp.float32) for _ in range(2)]
    span = lax.broadcasted_iota(jnp.int32, (SPANS, LANE), 0)
    entry = lax.broadcasted_iota(jnp.int32, (SPANS, LANE), 1)
    shift = (5 * rows * ((x * N + z) * N + y)) % 11
    for part in range(PIECE):
        line = span * PIECE + part
        number = 5 * (line // per_row) + 3 * ((line % per_row) * LANE + entry) + shift
        number = number.astype(jnp.float32)
        pattern = number - 11.0 * jnp.floor((number + 0.5) * (1.0 / 11.0))
        weight = 1.0 + pattern * 0.1
        for t in range(2):
            totals[t] += piece_lines(t * PIECE + part) * weight
    scale = 1.0 / math.sqrt(N * PLANE * PIECE * LANE)
    ones = jnp.ones((8, LANE), jnp.float32)
    sums[...] = jnp.zeros_like(sums)
    for t in range(2):
        row = scale * lax.dot_general(
            ones,
            totals[t],
            (((1,), (1,)), ((), ())),
            precision=lax.Precision.HIGHEST,
            preferred_element_type=jnp.float32,
        )
        for half in range(2):
            sums[2 * t + half : 2 * t + half + 1, :] = row[0:1, half * LANE : (half + 1) * LANE]
    sums_z[z] = sums[...]
    sum_line = [
        send(sums, sums_z.at[z], s_send.at[s - 1], s_recv.at[s - 1], line_id(s))
        for s in range(1, N)
    ]

    place_col = jnp.sum(jnp.where(same_z & (col_id < row_id), 1, 0), axis=1, keepdims=True)
    same_w = (w_col == w_row) & (row_id // (N * PLANE) == col_id // (N * PLANE))
    slot_col = jnp.sum(jnp.where(same_w & (col_id < row_id), 1, 0), axis=1, keepdims=True)
    round_col = lax.broadcasted_iota(jnp.int32, (SPANS, 1), 0) // (N * PLANE)
    writer_col = (w_col // PLANE) * N + w_col % N
    value_col = writer_col * (2 * SLOTS) + round_col * MOST + slot_col
    lane = lax.broadcasted_iota(jnp.int32, (SPANS, 2 * room), 1)
    second_half = lane >= room
    found = (z_col == z) & (place_col == jnp.where(second_half, lane - room, lane))
    value = value_col + jnp.where(second_half, SLOTS, 0)
    target = jnp.sum(jnp.where(found, value + 1, 0), axis=0, keepdims=True) - 1
    wide = lax.broadcasted_iota(jnp.int32, (2 * SLOTS * PLANE, 2 * room), 0)
    by_writer = (wide == target).astype(jnp.float32).astype(jnp.bfloat16)

    home = pl.ds(pl.multiple_of((y * N + x) * BLOCK, 8), BLOCK)
    planes, keeps, sum_plane, sum_expert = [], [], [], []
    for part in range(PARTS):
        if part + AHEAD < PARTS:
            pack(part + AHEAD)
        for copy in lines[3 * part : 3 * part + 3]:
            copy.wait_recv()
        if part + AHEAD < PARTS:
            send_line(part + AHEAD)
        owns[part].wait()
        if part == 1:
            for copy in sum_line:
                copy.wait_recv()
            line_sum[...] = sums_z[0] + sums_z[1] + sums_z[2] + sums_z[3]
            sums_p[here] = line_sum[...]
            for s in range(1, PLANE):
                at = N - 2 + s
                sum_plane.append(
                    send(line_sum, sums_p.at[here], s_send.at[at], s_recv.at[at], plane_id(s))
                )
        if part == 6:
            for copy in sum_plane:
                copy.wait_recv()
            total = sums_p[0]
            for d in range(1, PLANE):
                total = total + sums_p[d]
            plane_sum[...] = total
            sums_e[e_0 * 2 + e_1] = total
            for s in range(1, N):
                at = N + PLANE - 3 + s
                sum_expert.append(
                    send(
                        plane_sum,
                        sums_e.at[e_0 * 2 + e_1],
                        s_send.at[at],
                        s_recv.at[at],
                        expert_id(s),
                    )
                )
        for half in range(2):
            got = select_rows(by_writer, near[part, 2 * room * half : 2 * room * (half + 1), :])
            at = slice(2 * SLOTS * half, 2 * SLOTS * (half + 1))
            ready[part, :, at, :] = got.reshape(PLANE, 2 * SLOTS, LANE)
        for i in range(PLANE - 1):
            s = 1 + (i + 4 * part) % (PLANE - 1)
            to_x, to_y = in_plane(s)
            planes.append(
                send(
                    ready.at[part, to_x * N + to_y],
                    out.at[part, home],
                    p_send.at[part, s - 1],
                    p_recv.at[part, s - 1],
                    plane_id(s),
                )
            )
        keep = pltpu.make_async_copy(ready.at[part, here], out.at[part, home], keep_sem.at[part])
        keep.start()
        keeps.append(keep)

    for copy in sum_expert:
        copy.wait_recv()
    sums_out[...] = sums_e[...]
    for copy in keeps:
        copy.wait()
    for copy in lines + sum_line + sum_plane + sum_expert:
        copy.wait_send()
    for copy in planes:
        copy.wait()


def unpack(got, sums, file_slot, saved_m, saved_u, checks, lines, full_m, full_u, both, in_sem, out_sem):
    copies = []
    for part in range(PARTS):
        copy = pltpu.make_async_copy(got.at[part], lines.at[part], in_sem.at[part])
        copy.start()
        copies.append(copy)

    for g in range(N):
        for i in range(2):
            for half in range(2):
                both[2 * g + i : 2 * g + i + 1, half * LANE : (half + 1) * LANE] = sums[
                    g, 2 * i + half : 2 * i + half + 1, :
                ]
    slot_id = lax.broadcasted_iota(jnp.int32, (SPANS, SPANS), 0)
    placing = (file_slot[...] == slot_id).astype(jnp.float32)
    placed = lax.dot_general(
        both[...],
        placing,
        (((1,), (1,)), ((), ())),
        precision=lax.Precision.HIGHEST,
        preferred_element_type=jnp.float32,
    )
    for g in range(N):
        checks[g] = placed[2 * g : 2 * g + 2, :]

    def move_lines(part, slot, full):
        for at_y in range(N):
            rows = lines[part, pl.ds(at_y * N * BLOCK + slot, PLANE, stride=SLOTS), :]
            full[slot, pl.ds(at_y * PIECE + part % PIECE, PLANE, stride=N * PIECE), :] = rows

    outs = []
    for part in range(PIECE):
        copies[part].wait()
        for slot in range(SLOTS):
            move_lines(part, slot, full_m)
    copy = pltpu.make_async_copy(full_m, saved_m, out_sem.at[SLOTS])
    copy.start()
    outs.append(copy)
    for part in range(PIECE, PARTS):
        copies[part].wait()
    for slot in range(SLOTS):
        for part in range(PIECE, PARTS):
            move_lines(part, slot, full_u)
        copy = pltpu.make_async_copy(full_u.at[slot], saved_u.at[slot], out_sem.at[slot])
        copy.start()
        outs.append(copy)
    for copy in outs:
        copy.wait()


SMEM = pl.BlockSpec(memory_space=pltpu.SMEM)
VMEM = pl.BlockSpec(memory_space=pltpu.VMEM)
ANY = pl.BlockSpec(memory_space=pl.ANY)
F32 = jnp.float32


def move(room, number, master, first, second, rotation):
    rows, cols = master.shape
    lines = rows * cols // LANE
    small = 2 * (N - 1) + PLANE - 1
    return pl.pallas_call(
        functools.partial(exchange, room),
        out_shape=(
            jax.ShapeDtypeStruct((PARTS, PLANE * BLOCK, LANE), F32),
            jax.ShapeDtypeStruct((N, 8, LANE), F32),
        ),
        in_specs=[ANY, ANY, ANY, VMEM],
        out_specs=(ANY, VMEM),
        scratch_shapes=[
            pltpu.VMEM((rows, cols), F32),
            pltpu.VMEM((rows, cols), F32),
            pltpu.VMEM((rows, cols), F32),
            pltpu.VMEM((8, SPANS), jnp.int32),
            pltpu.VMEM((lines, LANE), F32),
            pltpu.VMEM((lines, LANE), F32),
            pltpu.VMEM((PARTS, N * room, LANE), F32),
            pltpu.VMEM((PARTS, N * room, LANE), F32),
            pltpu.VMEM((PARTS, PLANE, BLOCK, LANE), F32),
            pltpu.VMEM((8, LANE), F32),
            pltpu.VMEM((N, 8, LANE), F32),
            pltpu.VMEM((PLANE, 8, LANE), F32),
            pltpu.VMEM((N, 8, LANE), F32),
            pltpu.VMEM((8, LANE), F32),
            pltpu.VMEM((8, LANE), F32),
            pltpu.SemaphoreType.DMA((3,)),
            pltpu.SemaphoreType.DMA((PARTS,)),
            pltpu.SemaphoreType.DMA((PARTS,)),
            pltpu.SemaphoreType.DMA((PARTS, N - 1)),
            pltpu.SemaphoreType.DMA((PARTS, N - 1)),
            pltpu.SemaphoreType.DMA((PARTS, PLANE - 1)),
            pltpu.SemaphoreType.DMA((PARTS, PLANE - 1)),
            pltpu.SemaphoreType.DMA((small,)),
            pltpu.SemaphoreType.DMA((small,)),
        ],
        compiler_params=pltpu.CompilerParams(collective_id=number, has_side_effects=True),
    )(master, first, second, rotation)


def shards(master, first, second, rotation, assignment):
    rotation = rotation.reshape(ROUNDS, N * PLANE)
    fits = pl.pallas_call(
        plane_load,
        out_shape=jax.ShapeDtypeStruct((1,), jnp.int32),
        in_specs=[VMEM],
        out_specs=SMEM,
    )(rotation)
    got, sums = lax.cond(
        fits[0] > 0,
        functools.partial(move, USUAL, 0),
        functools.partial(move, ALL, 1),
        master[0],
        first[0],
        second[0],
        rotation,
    )
    length = N * PLANE * PIECE
    saved_m, saved_u, checks = pl.pallas_call(
        unpack,
        out_shape=(
            jax.ShapeDtypeStruct((SLOTS, length, LANE), F32),
            jax.ShapeDtypeStruct((SLOTS, length, LANE), F32),
            jax.ShapeDtypeStruct((N, 2, SPANS), F32),
        ),
        in_specs=[ANY, VMEM, VMEM],
        out_specs=(ANY, ANY, VMEM),
        scratch_shapes=[
            pltpu.VMEM((PARTS, PLANE * BLOCK, LANE), F32),
            pltpu.VMEM((SLOTS, length, LANE), F32),
            pltpu.VMEM((SLOTS, length, LANE), F32),
            pltpu.VMEM((2 * N, SPANS), F32),
            pltpu.SemaphoreType.DMA((PARTS,)),
            pltpu.SemaphoreType.DMA((SLOTS + 1,)),
        ],
    )(got, sums, assignment.reshape(1, SPANS))
    shape = (1, ROUNDS, MOST, length, LANE)
    return saved_m.reshape(shape), saved_u.reshape(shape), checks


def solution(mesh):
    torus = Mesh(mesh.devices.reshape(N, N, N, 2, 2), DP + EXPERT)
    rows = P(EXPERT, DP, None)
    saved = P(EXPERT, DP, None, None, None)
    return jax.shard_map(
        shards,
        mesh=torus,
        in_specs=(rows, rows, rows, P(), P()),
        out_specs=(saved, saved, P()),
        check_vma=False,
    )
```

time: 124 us -> 96.7 us (0.78)
  Pallas kernels: 116 us -> 94.5 us
  local copies, waits for them, and re-layouts: 5.01 us -> 0 us
  other arithmetic: 2.12 us -> 0 us
    pallas_call x1, Pallas kernels: 101 us -> 87.5 us  [move(): pl.pallas_call(functools.partial(exchange, room), out_shape=(jax.ShapeDty...]
    pallas_call x1, Pallas kernels: 6.76 us -> 1.34 us  [shards(): pl.pallas_call(plane_load, out_shape=jax.ShapeDtypeStruct((1,), jnp.int32...]
    reshape x5 -> x0, local copies, waits for them, and re-layouts: 3.7 us -> none  [the longest x1 1.3 us: shards(): checks.reshape(N, 2, SPANS)]
    pallas_call x1, Pallas kernels: 7.68 us -> 5.66 us  [shards(): pl.pallas_call(unpack, out_shape=(jax.ShapeDtypeStruct((SLOTS, length, LA...]
    unnamed x1 -> x0, other arithmetic: 1.34 us -> none
where the time goes in v2:
time: 96.7 us; the launch traced here: 96.5 us
  Pallas kernels  94.5 us (98%)
  between operations  1.51 us (2%)
    pallas_call x1, Pallas kernels, move(): pl.pallas_call(functools.partial(exchange, room), out_shape=(jax.ShapeDty...  87.5 us
    pallas_call x1, Pallas kernels, shards(): pl.pallas_call(unpack, out_shape=(jax.ShapeDtypeStruct((SLOTS, length, LA...  5.66 us

profile of v2, /device:TPU:32, one launch (start us, length us, event | category | flops | bytes accessed | tf_op | source)
XLA Modules:
  0.0 96.5 jit_solution(11616627236810072209)
XLA Ops:
  0.6 1.3 %shard_map.76 = s32[1]{0:T(128)} custom-call(s32[4,64]{1,0:T(4,128)} %bitcast.14), custom_call_target="tpu_custom_call" | custom-call | tf_op jit(solution)/shard_map/pallas_call | solution.py:415
  2.6 88.0 %conditional.1 = ((f32[14,768,128]{2,1,0:T(8,128)}, f32[4,8,128]{2,1,0:T(8,128)S(1)})) conditional(s32[]{:T(128)} %bitcast.1, (f32[112,2048]{1,0:T(8,128)}, f32[112,2048]{1,0:T(8,128)}, f32[112,2048]{1,0:T(8,128)}, s32[4,64]{1,0:T(4,128)}) %tuple.26, (f32[112,2048]{1,0:T(8,128)}, f32[112,2048]{1,0:T(8,128)}, f32[112,2048]{1,0:T(8,128)}, ...), branch_computations={%region_0.0_spmd, %region_1.0_spmd} | conditional | bytes 8 | solution.py:421
  2.9 87.5 %branch_1_fun.1 = (f32[14,768,128]{2,1,0:T(8,128)}, f32[4,8,128]{2,1,0:T(8,128)S(1)}) custom-call(f32[112,2048]{1,0:T(8,128)} %get-tuple-element.20.master, f32[112,2048]{1,0:T(8,128)} %get-tuple-element.21.first, f32[112,2048]{1,0:T(8,128)} %get-tuple-element.22.second, s32[4,64]{1,0:T(4,128)} %get-tuple-element.23.rotation), custom_call_target="tpu_custom_call" | custom-call | tf_op jit(solution)/shard_map/cond/branch_1_fun/pallas_call | solution.py:375
  90.7 5.7 %shard_map.77 = (f32[12,448,128]{2,1,0:T(8,128)}, f32[12,448,128]{2,1,0:T(8,128)}, f32[4,2,256]{2,1,0:T(2,128)}) custom-call(f32[14,768,128]{2,1,0:T(8,128)} %get-tuple-element.32.got, f32[4,8,128]{2,1,0:T(8,128)S(1)} %get-tuple-element.33.sums, s32[1,256]{1,0:T(1,128)} %bitcast.17), custom_call_target="tpu_custom_call" | custom-call | tf_op jit(solution)/shard_map/pallas_call | solution.py:431
